TPU v7x, 32 devices: a whole 2x2x4 slice. The times are simulated.
32 devices in a mesh: section: 2 (over x), tensor: 4 (over z), dp: 4 (over y, core).
Axes of the slice: x: 2, y: 2, z: 4, core: 2. Of those that a mesh axis runs over, the one named last changes fastest.
Arguments:
- tokens: bfloat16 [16, 4096], P(None, ('section', 'dp')), may hold values from -100 to 100
- attn_gain: float32 [4096], P(('section', 'dp')), may hold values from 0.1 to 1.9
- qkv_weight: bfloat16 [4096, 10240], P(('section', 'dp'), 'tensor'), may hold values from -0.09375 to 0.09375
- qkv_order: int32 [10], replicated, may hold values from 0 to 9, each once
- cache_keys: bfloat16 [16, 8, 4096, 128], P(('section', 'dp'), 'tensor'), may hold values from -1300 to 1300
- cache_values: bfloat16 [16, 8, 4096, 128], P(('section', 'dp'), 'tensor'), may hold values from -6 to 6
- cache_len: int32 [16], P(('section', 'dp')), may hold values from 2 to 4096, as said below
- out_weight: bfloat16 [8192, 4096], P('tensor', ('section', 'dp')), may hold values from -0.0625 to 0.0625
- ffn_gain: float32 [4096], P(('section', 'dp')), may hold values from 0.1 to 1.9
- gate_up: bfloat16 [2, 4096, 28672], P(None, ('section', 'dp'), 'tensor'), may hold values from -0.09375 to 0.09375
- down_weight: bfloat16 [28672, 4096], P('tensor', ('section', 'dp')), may hold values from -0.03125 to 0.03125
Outputs:
- layer_out: bfloat16 [16, 4096], P(None, ('section', 'dp'))
Inputs may be any that keep to these rules, and one draw needn't show every extreme that they name: qkv_order is a permutation of 0 to 9, the same for every key-value group. `cache_len`: at least one sequence has all 4096 positions valid.
All inputs are finite; a program needn't handle non-finite values.
Results may differ from a plain program's by a relative error of at most 0.0065.
Values may be sent and summed in bfloat16 or wider, within the bound.
A program may use at most 64 MiB of HBM per device.

v0:
```python
import jax
import jax.numpy as jnp
from jax import lax
from jax.sharding import PartitionSpec as P

D = 4096
HEADS = 64
KV_HEADS = 8
HD = 128
LEN = 4096
GROUP = 10


def normalize(stream, gain_vec):
    wide = stream.astype(jnp.float32)
    squares = lax.psum(jnp.sum(wide * wide, axis=1), ("section", "dp"))
    factor = lax.rsqrt(squares / D + 1e-05)
    return (wide * factor[:, None] * gain_vec[None, :]).astype(jnp.bfloat16)


def rotate(vector, cosine, sine_part):
    half_dim = vector.shape[-1] // 2
    first_half = vector[..., :half_dim]
    second = vector[..., half_dim:]
    return jnp.concatenate(
        [first_half * cosine - second * sine_part, second * cosine + first_half * sine_part],
        axis=-1,
    )


def project_rows(row_block, weight_cols):
    return jnp.dot(
        lax.all_gather(row_block, ("section", "dp"), axis=0, tiled=True),
        weight_cols,
        preferred_element_type=jnp.float32,
    )


def add_residual(base_rows, partial_sum):
    summed = lax.psum(partial_sum, "tensor")
    return (base_rows.astype(jnp.float32) + summed).astype(jnp.bfloat16)


def body(
    tokens,
    attn_gain,
    qkv_weight,
    qkv_order,
    cache_keys,
    cache_values,
    cache_len,
    out_weight,
    ffn_gain,
    gate_up,
    down_weight,
):
    seq_count = cache_len.shape[0]
    local_groups = cache_keys.shape[1]
    per_group = HEADS // KV_HEADS
    normed = normalize(tokens, attn_gain)
    row_block = normed
    joined_cols = lax.psum_scatter(
        jnp.dot(row_block, qkv_weight, preferred_element_type=jnp.float32),
        ("section", "dp"),
        scatter_dimension=0,
        tiled=True,
    )
    blocks = joined_cols.reshape(seq_count, local_groups, GROUP, HD)
    onehot = (qkv_order[:, None] == jnp.arange(GROUP, dtype=jnp.int32)[None, :]).astype(jnp.float32)
    logical = jnp.einsum("bgjd,ji->bgid", blocks, onehot, precision=lax.Precision.HIGHEST)
    half_dim = HD // 2
    inv_freq = 500000.0 ** (-(2.0 * jnp.arange(half_dim, dtype=jnp.float32)) / HD)
    angles = cache_len.astype(jnp.float32)[:, None] * inv_freq[None, :]
    cosine = jnp.cos(angles)
    sine_part = jnp.sin(angles)
    queries = rotate(
        logical[:, :, :per_group], cosine[:, None, None, :], sine_part[:, None, None, :]
    ).astype(jnp.bfloat16)
    new_key = rotate(logical[:, :, per_group], cosine[:, None, :], sine_part[:, None, :]).astype(
        jnp.bfloat16
    )
    new_value = logical[:, :, per_group + 1].astype(jnp.bfloat16)
    inv_scale = 1.0 / jnp.sqrt(jnp.float32(HD))
    scores = (
        jnp.einsum("bgpd,bgld->bgpl", queries, cache_keys, preferred_element_type=jnp.float32)
        * inv_scale
    )
    own_score = (
        jnp.einsum("bgpd,bgd->bgp", queries, new_key, preferred_element_type=jnp.float32)
        * inv_scale
    )
    valid_mask = jnp.arange(LEN, dtype=jnp.int32)[None, :] < cache_len[:, None]
    masked = jnp.where(valid_mask[:, None, None, :], scores, -jnp.inf)
    peak = jnp.maximum(jnp.max(masked, axis=-1), own_score)
    weights = jnp.exp(masked - peak[..., None])
    own_weight = jnp.exp(own_score - peak)
    denom_sum = jnp.sum(weights, axis=-1) + own_weight
    probabilities = (weights / denom_sum[..., None]).astype(jnp.bfloat16)
    own_prob = (own_weight / denom_sum).astype(jnp.bfloat16)
    mixed_heads = jnp.einsum(
        "bgpl,bgld->bgpd", probabilities, cache_values, preferred_element_type=jnp.float32
    )
    mixed_heads = (
        mixed_heads
        + own_prob.astype(jnp.float32)[..., None] * new_value.astype(jnp.float32)[:, :, None, :]
    )
    attended = mixed_heads.astype(jnp.bfloat16).reshape(seq_count, -1)
    hidden_state = add_residual(tokens, project_rows(attended, out_weight))
    ffn_normed = normalize(hidden_state, ffn_gain)
    row_block = ffn_normed
    gate_and_up = lax.psum_scatter(
        jnp.einsum("rd,kdf->rkf", row_block, gate_up, preferred_element_type=jnp.float32),
        ("section", "dp"),
        scatter_dimension=0,
        tiled=True,
    )
    activated = (jax.nn.silu(gate_and_up[:, 0]) * gate_and_up[:, 1]).astype(jnp.bfloat16)
    return add_residual(hidden_state, project_rows(activated, down_weight))


def solution(mesh):
    return jax.shard_map(
        body,
        mesh=mesh,
        in_specs=(
            P(None, ("section", "dp")),
            P(("section", "dp")),
            P(("section", "dp"), "tensor"),
            P(),
            P(("section", "dp"), "tensor", None, None),
            P(("section", "dp"), "tensor", None, None),
            P(("section", "dp")),
            P("tensor", ("section", "dp")),
            P(("section", "dp")),
            P(None, ("section", "dp"), "tensor"),
            P("tensor", ("section", "dp")),
        ),
        out_specs=P(None, ("section", "dp")),
        check_vma=False,
    )
```

profile of v0, /device:TPU:0, one launch (start us, length us, event | category | flops | bytes accessed | tf_op | source)
XLA Modules:
  0.0 227.4 jit_solution(6629242835967836412)
XLA Ops:
  6.5 0.0 copy-start
  6.5 0.0 all-reduce.5.cloned.1.call-start
  6.5 1.0 fusion.7
  7.5 15.1 %psum.28 = f32[16]{0:T(128)S(1)} all-reduce(f32[16]{0:T(128)S(1)} %fusion.7), channel_id=1, replica_groups=mesh['section'=2,'tensor'=4,'dp'=4] {'section','dp'}, use_global_device_ids=true, to_apply=%region_1.0 | all-reduce | flops 16 | bytes 128 | tf_op jit(solution)/shard_map/psum | solution.py:16
  22.7 0.0 copy-done
  22.7 1.9 fusion.19
  24.6 0.0 all-reduce.5.cloned.1.call-update
  24.6 0.0 all-reduce.7.cloned.1.call-start
  24.6 0.7 convert_element_type.47
  25.3 0.7 iota_compare_fusion
  26.0 0.1 multiply_cosine_fusion
  26.2 1.2 dynamic-slice
  28.1 48.3 %all-reduce.5.cloned.1.call-done = f32[16,2560]{1,0:T(8,128)} async-done(((f32[16,2560]{1,0:T(8,128)}), f32[16,2560]{1,0:T(8,128)}) %all-reduce.5.cloned.1.call-update) | async-done | bytes 163856
  76.4 0.9 constant_dynamic-slice_fusion
  77.3 0.0 copy-start.1
  77.3 0.9 convolution_bitcast_fusion
  78.3 0.1 subtract_convert_fusion
  78.4 0.1 subtract_convert_fusion.1
  78.5 0.1 maximum_bitcast_fusion
  78.5 0.2 fusion.29
  78.7 3.5 %fusion.36 = (f32[2,2,8]{2,1,0:T(2,128)S(1)}, f32[2,2,8,4096]{3,2,1,0:T(8,128)S(1)}) fusion(bf16[2,2,4096,128]{3,2,1,0:T(8,128)(2,1)} %param.15, bf16[2,2,8,64]{3,2,1,0:T(8,128)(2,1)S(1)} %get-tuple-element.8, bf16[2,2,8,64]{3,2,1,0:T(8,128)(2,1)S(1)} %get-tuple-element.7, pred[2,4096]{1,0:T(4,128)(4,1)S(1)} %iota_compare_fusion), kind=kOutput, calls=%fused_computation.64 | convolution fusion | flops 33964000 | bytes 4735104 | tf_op jit(solution)/shard_map/bgpd,bgld->bgpl/dot_general | solution.py:85
  82.2 0.0 copy-start.2
  82.2 0.0 copy-start.3
  82.3 0.2 fusion.2
  82.5 0.0 copy-done.1
  82.5 0.7 fusion.1
  83.3 10.0 %all-gather = bf16[8,2,2048]{2,1,0:T(2,128)(2,1)S(1)} all-gather(bf16[1,2,2048]{2,1,0:T(2,128)(2,1)S(1)} %reshape.129), channel_id=1, replica_groups=mesh['section'=2,'tensor'=4,'dp'=4] {'section','dp'}, dimensions={0}, use_global_device_ids=true | all-gather | bytes 73728 | tf_op jit(solution)/shard_map/all_gather | solution.py:33
  93.3 2.0 fusion.37
  95.3 19.0 %psum.29 = f32[16,512]{1,0:T(8,128)S(1)} all-reduce(f32[16,512]{1,0:T(8,128)S(1)} %fusion.37), channel_id=1, replica_groups=mesh['section'=2,'tensor'=4,'dp'=4] {'tensor'}, use_global_device_ids=true, to_apply=%region_5.6 | all-reduce | flops 8192 | bytes 65536 | tf_op jit(solution)/shard_map/psum | solution.py:40
  114.3 0.0 copy-done.2
  114.3 0.1 fusion.11
  114.4 11.8 %psum.30 = f32[16]{0:T(128)S(1)} all-reduce(f32[16]{0:T(128)S(1)} %get-tuple-element.5), channel_id=1, replica_groups=mesh['section'=2,'tensor'=4,'dp'=4] {'section','dp'}, use_global_device_ids=true, to_apply=%region_7.8 | all-reduce | flops 16 | bytes 128 | tf_op jit(solution)/shard_map/psum | solution.py:16
  126.2 0.0 copy-done.3
  126.2 8.2 %fusion.17 = f32[16,2,7168]{2,0,1:T(8,128)} fusion(bf16[2,512,7168]{2,1,0:T(8,128)(2,1)} %param.20, bf16[16,512]{1,0:T(8,128)(2,1)S(1)} %get-tuple-element.6, f32[512]{0:T(512)S(1)} %copy-done.3, f32[16]{0:T(128)S(1)} %add_rsqrt_fusion), kind=kOutput, calls=%fused_computation.32 | convolution fusion | flops 234913792 | bytes 15616064 | tf_op jit(solution)/shard_map/rd,kdf->rkf/dot_general | solution.py:112
  134.4 0.0 all-reduce.7.cloned.1.call-update
  134.4 52.6 %all-reduce.7.cloned.1.call-done = f32[16,2,7168]{2,0,1:T(8,128)} async-done(((f32[16,2,7168]{2,0,1:T(8,128)}), f32[16,2,7168]{2,0,1:T(8,128)}) %all-reduce.7.cloned.1.call-update) | async-done | bytes 917520
  187.1 1.1 fusion.15
  188.2 8.6 %all-gather.1 = bf16[8,2,7168]{2,1,0:T(2,128)(2,1)S(1)} all-gather(bf16[1,2,7168]{2,1,0:T(2,128)(2,1)S(1)} %fusion.15), channel_id=1, replica_groups=mesh['section'=2,'tensor'=4,'dp'=4] {'section','dp'}, dimensions={0}, use_global_device_ids=true | all-gather | bytes 258048 | tf_op jit(solution)/shard_map/all_gather | solution.py:33
  196.8 0.1 reshape.132
  196.8 4.1 %fusion.38 = f32[16,512]{1,0:T(8,128)S(1)} fusion(bf16[16,7168]{1,0:T(8,128)(2,1)S(1)} %reshape.132, bf16[7168,512]{1,0:T(8,128)(2,1)} %param.21), kind=kOutput, calls=%fused_computation.66 | convolution fusion | flops 117440512 | bytes 7602176 | tf_op jit(solution)/shard_map/dot_general | solution.py:32
  201.0 19.0 %psum.31 = f32[16,512]{1,0:T(8,128)S(1)} all-reduce(f32[16,512]{1,0:T(8,128)S(1)} %fusion.38), channel_id=1, replica_groups=mesh['section'=2,'tensor'=4,'dp'=4] {'tensor'}, use_global_device_ids=true, to_apply=%region_9.10 | all-reduce | flops 8192 | bytes 65536 | tf_op jit(solution)/shard_map/psum | solution.py:40
  220.0 0.6 fusion.14
  (10 shorter events, 0.1 us)
Async XLA Ops:
  6.5 16.1 %copy-start = (bf16[512,2560]{1,0:T(8,128)(2,1)S(1)}, bf16[512,2560]{1,0:T(8,128)(2,1)}, u32[]{:S(2)}) copy-start(bf16[512,2560]{1,0:T(8,128)(2,1)} %param.13) | copy-start | bytes 7864324
  6.5 69.9 %all-reduce.5.cloned.1.call-start = ((), (), s32[]{:S(2)}) async-start(), calls=%async_computation | async-start | bytes 327680
  24.6 162.5 %all-reduce.7.cloned.1.call-start = ((), (), s32[]{:S(2)}) async-start(), calls=%async_computation.1 | async-start | bytes 1835008
  77.3 5.2 %copy-start.1 = (bf16[2,2,4096,128]{3,2,1,0:T(8,128)(2,1)S(1)}, bf16[2,2,4096,128]{3,2,1,0:T(8,128)(2,1)}, u32[]{:S(2)}) copy-start(bf16[2,2,4096,128]{3,2,1,0:T(8,128)(2,1)} %param.16) | copy-start | bytes 12582916
  82.2 32.0 %copy-start.2 = (bf16[16,512]{1,0:T(8,128)(2,1)S(1)}, bf16[16,512]{1,0:T(8,128)(2,1)}, u32[]{:S(2)}) copy-start(bf16[16,512]{1,0:T(8,128)(2,1)} %param.11) | copy-start | bytes 49156
  82.2 44.0 %copy-start.3 = (f32[512]{0:T(512)S(1)}, f32[512]{0:T(512)}, u32[]{:S(2)}) copy-start(f32[512]{0:T(512)} %param.19) | copy-start | bytes 6148
Sparse Core Ops, SparseCore 0:
  24.7 51.6 all-reduce.4
  134.6 52.4 all-reduce.6
where the time goes:
time: 228 us; the launch traced here: 227 us
  waiting for transfers between devices  101 us (44%)
  blocking collectives  83.5 us (37%)
  matrix products  21.5 us (9%)
  between operations  14.2 us (6%)
  other arithmetic  4.91 us (2%)
  local copies, waits for them, and re-layouts  2.31 us (1%)
    unnamed x4, waiting for transfers between devices  101 us
    psum x2, blocking collectives, add_residual(): summed = lax.psum(partial_sum, 'tensor')  38 us
    psum x2, blocking collectives, normalize(): squares = lax.psum(jnp.sum(wide * wide, axis=1), ('section', 'dp'))  27 us
    all_gather x2, blocking collectives, project_rows(): lax.all_gather(row_block, ('section', 'dp'), axis=0, tiled=True)  18.6 us
    dot_general x1, matrix products, body(): jnp.einsum('rd,kdf->rkf', row_block, gate_up, preferred_element_type=jnp....  8.21 us
    dot_general x2, matrix products, project_rows(): jnp.dot(lax.all_gather(row_block, ('section', 'dp'), axis=0, tiled=True),...  6.09 us
  transfers between devices with their start and end apart: 2, of which 2 were waited for; matrix products, arithmetic and copies ran while one was open for 1% of the time, Pallas kernels for 0%

commit v1 on v0

--- a/solution.py
+++ b/solution.py
@@ -37,7 +37,9 @@
 
 
 def add_residual(base_rows, partial_sum):
-    summed = lax.psum(partial_sum, "tensor")
+    summed = partial_sum
+    for hop in (1, 2):
+        summed = summed + lax.ppermute(summed, "tensor", [(dev, dev ^ hop) for dev in range(4)])
     return (base_rows.astype(jnp.float32) + summed).astype(jnp.bfloat16)
 
 

time: 228 us -> 210 us (0.921)
  blocking collectives: 83.5 us -> 45.5 us
  waiting for transfers between devices: 101 us -> 114 us
  starting transfers between devices: 0.04 us -> 7.86 us
    psum x2 -> x0, blocking collectives: 38 us -> none  [add_residual(): summed = lax.psum(partial_sum, 'tensor')]
    ppermute x0 -> x4, waiting for transfers between devices: none -> 9.67 us  [add_residual(): lax.ppermute(summed, 'tensor', [(dev, dev ^ hop) for dev in range(4)])]
    ppermute x0 -> x4, starting transfers between devices: none -> 7.81 us  [add_residual(): lax.ppermute(summed, 'tensor', [(dev, dev ^ hop) for dev in range(4)])]
    unnamed x4, waiting for transfers between devices: 101 us -> 104 us
  transfers between devices with their start and end apart: 2 -> 6, of which waited for: 2 -> 6; matrix products, arithmetic and copies ran while one was open for 1% -> 1% of each run, Pallas kernels for 0% -> 0%
where the time goes in v1:
time: 210 us
  waiting for transfers between devices  114 us (54%)
  blocking collectives  45.5 us (22%)
  matrix products  21.5 us (10%)
  between operations  14.2 us (7%)
  starting transfers between devices  7.86 us (4%)
  other arithmetic  4.93 us (2%)
  local copies, waits for them, and re-layouts  2.31 us (1%)
    unnamed x4, waiting for transfers between devices  104 us
    psum x2, blocking collectives, normalize(): squares = lax.psum(jnp.sum(wide * wide, axis=1), ('section', 'dp'))  27 us
    all_gather x2, blocking collectives, project_rows(): lax.all_gather(row_block, ('section', 'dp'), axis=0, tiled=True)  18.6 us
    ppermute x4, waiting for transfers between devices, add_residual(): lax.ppermute(summed, 'tensor', [(dev, dev ^ hop) for dev in range(4)])  9.67 us
    dot_general x1, matrix products, body(): jnp.einsum('rd,kdf->rkf', row_block, gate_up, preferred_element_type=jnp....  8.21 us
    ppermute x4, starting transfers between devices, add_residual(): lax.ppermute(summed, 'tensor', [(dev, dev ^ hop) for dev in range(4)])  7.81 us
    dot_general x2, matrix products, project_rows(): jnp.dot(lax.all_gather(row_block, ('section', 'dp'), axis=0, tiled=True),...  6.09 us
  transfers between devices with their start and end apart: 6, of which 6 were waited for; matrix products, arithmetic and copies ran while one was open for 1% of the time, Pallas kernels for 0%

profile of v1, /device:TPU:0, one launch (start us, length us, event | category | flops | bytes accessed | tf_op | source)
XLA Modules:
  0.0 210.0 jit_solution(15147693219271510701)
XLA Ops:
  6.5 0.0 copy-start
  6.5 0.0 all-reduce.5.cloned.1.call-start
  6.5 1.0 fusion.7
  7.5 15.1 %psum.14 = f32[16]{0:T(128)S(1)} all-reduce(f32[16]{0:T(128)S(1)} %fusion.7), channel_id=1, replica_groups=mesh['section'=2,'tensor'=4,'dp'=4] {'section','dp'}, use_global_device_ids=true, to_apply=%region_1.0 | all-reduce | flops 16 | bytes 128 | tf_op jit(solution)/shard_map/psum | solution.py:16
  22.7 0.0 copy-done
  22.7 1.9 fusion.19
  24.6 0.0 all-reduce.5.cloned.1.call-update
  24.6 0.0 all-reduce.7.cloned.1.call-start
  24.6 0.7 convert_element_type.47
  25.3 0.7 iota_compare_fusion
  26.0 0.1 multiply_cosine_fusion
  26.2 1.2 dynamic-slice
  28.1 48.3 %all-reduce.5.cloned.1.call-done = f32[16,2560]{1,0:T(8,128)} async-done(((f32[16,2560]{1,0:T(8,128)}), f32[16,2560]{1,0:T(8,128)}) %all-reduce.5.cloned.1.call-update) | async-done | bytes 163856
  76.4 0.9 constant_dynamic-slice_fusion
  77.3 0.0 copy-start.1
  77.3 0.9 convolution_bitcast_fusion
  78.3 0.1 subtract_convert_fusion
  78.4 0.1 subtract_convert_fusion.1
  78.5 0.1 maximum_bitcast_fusion
  78.5 0.2 fusion.29
  78.7 3.5 %fusion.36 = (f32[2,2,8]{2,1,0:T(2,128)S(1)}, f32[2,2,8,4096]{3,2,1,0:T(8,128)S(1)}) fusion(bf16[2,2,4096,128]{3,2,1,0:T(8,128)(2,1)} %param.15, bf16[2,2,8,64]{3,2,1,0:T(8,128)(2,1)S(1)} %get-tuple-element.8, bf16[2,2,8,64]{3,2,1,0:T(8,128)(2,1)S(1)} %get-tuple-element.7, pred[2,4096]{1,0:T(4,128)(4,1)S(1)} %iota_compare_fusion), kind=kOutput, calls=%fused_computation.64 | convolution fusion | flops 33964000 | bytes 4735104 | tf_op jit(solution)/shard_map/bgpd,bgld->bgpl/dot_general | solution.py:87
  82.2 0.0 copy-start.2
  82.2 0.0 copy-start.3
  82.3 0.2 fusion.2
  82.5 0.0 copy-done.1
  82.5 0.7 fusion.1
  83.3 10.0 %all-gather = bf16[8,2,2048]{2,1,0:T(2,128)(2,1)S(1)} all-gather(bf16[1,2,2048]{2,1,0:T(2,128)(2,1)S(1)} %reshape.129), channel_id=1, replica_groups=mesh['section'=2,'tensor'=4,'dp'=4] {'section','dp'}, dimensions={0}, use_global_device_ids=true | all-gather | bytes 73728 | tf_op jit(solution)/shard_map/all_gather | solution.py:33
  93.3 2.0 fusion.37
  95.3 1.5 collective-permute-start
  96.8 2.4 %collective-permute-done = f32[16,512]{1,0:T(8,128)S(1)} collective-permute-done((f32[16,512]{1,0:T(8,128)S(1)}, f32[16,512]{1,0:T(8,128)S(1)}, u32[]{:S(2)}, u32[]{:S(2)}) %collective-permute-start) | collective-permute-done | bytes 32800 | tf_op jit(solution)/shard_map/ppermute | solution.py:42
  99.2 2.4 %collective-permute-start.1 = (f32[16,512]{1,0:T(8,128)S(1)}, f32[16,512]{1,0:T(8,128)S(1)}, u32[]{:S(2)}, u32[]{:S(2)}) collective-permute-start(f32[16,512]{1,0:T(8,128)S(1)} %add.53), channel_id=1, source_target_pairs={{0,8},{4,12},{8,0},{12,4},{1,9},{5,13},{9,1},{13,5},{2,10},{6,14},... | collective-permute-start | bytes 98312 | tf_op jit(solution)/shard_map/ppermute | solution.py:42
  101.6 2.4 %collective-permute-done.1 = f32[16,512]{1,0:T(8,128)S(1)} collective-permute-done((f32[16,512]{1,0:T(8,128)S(1)}, f32[16,512]{1,0:T(8,128)S(1)}, u32[]{:S(2)}, u32[]{:S(2)}) %collective-permute-start.1) | collective-permute-done | bytes 32800 | tf_op jit(solution)/shard_map/ppermute | solution.py:42
  104.0 0.0 copy-done.2
  104.0 0.1 fusion.11
  104.1 11.8 %psum.15 = f32[16]{0:T(128)S(1)} all-reduce(f32[16]{0:T(128)S(1)} %get-tuple-element.5), channel_id=1, replica_groups=mesh['section'=2,'tensor'=4,'dp'=4] {'section','dp'}, use_global_device_ids=true, to_apply=%region_6.7 | all-reduce | flops 16 | bytes 128 | tf_op jit(solution)/shard_map/psum | solution.py:16
  116.0 0.0 copy-done.3
  116.0 8.2 %fusion.17 = f32[16,2,7168]{2,0,1:T(8,128)} fusion(bf16[2,512,7168]{2,1,0:T(8,128)(2,1)} %param.20, bf16[16,512]{1,0:T(8,128)(2,1)S(1)} %get-tuple-element.6, f32[512]{0:T(512)S(1)} %copy-done.3, f32[16]{0:T(128)S(1)} %add_rsqrt_fusion), kind=kOutput, calls=%fused_computation.32 | convolution fusion | flops 234913792 | bytes 15616064 | tf_op jit(solution)/shard_map/rd,kdf->rkf/dot_general | solution.py:114
  124.2 0.0 all-reduce.7.cloned.1.call-update
  124.2 55.7 %all-reduce.7.cloned.1.call-done = f32[16,2,7168]{2,0,1:T(8,128)} async-done(((f32[16,2,7168]{2,0,1:T(8,128)}), f32[16,2,7168]{2,0,1:T(8,128)}) %all-reduce.7.cloned.1.call-update) | async-done | bytes 917520
  179.9 1.1 fusion.15
  181.0 8.6 %all-gather.1 = bf16[8,2,7168]{2,1,0:T(2,128)(2,1)S(1)} all-gather(bf16[1,2,7168]{2,1,0:T(2,128)(2,1)S(1)} %fusion.15), channel_id=1, replica_groups=mesh['section'=2,'tensor'=4,'dp'=4] {'section','dp'}, dimensions={0}, use_global_device_ids=true | all-gather | bytes 258048 | tf_op jit(solution)/shard_map/all_gather | solution.py:33
  189.6 0.1 reshape.132
  189.7 4.1 %fusion.38 = f32[16,512]{1,0:T(8,128)S(1)} fusion(bf16[16,7168]{1,0:T(8,128)(2,1)S(1)} %reshape.132, bf16[7168,512]{1,0:T(8,128)(2,1)} %param.21), kind=kOutput, calls=%fused_computation.66 | convolution fusion | flops 117440512 | bytes 7602176 | tf_op jit(solution)/shard_map/dot_general | solution.py:32
  193.8 1.5 collective-permute-start.2
  195.3 2.4 %collective-permute-done.2 = f32[16,512]{1,0:T(8,128)S(1)} collective-permute-done((f32[16,512]{1,0:T(8,128)S(1)}, f32[16,512]{1,0:T(8,128)S(1)}, u32[]{:S(2)}, u32[]{:S(2)}) %collective-permute-start.2) | collective-permute-done | bytes 32800 | tf_op jit(solution)/shard_map/ppermute | solution.py:42
  197.7 2.4 %collective-permute-start.3 = (f32[16,512]{1,0:T(8,128)S(1)}, f32[16,512]{1,0:T(8,128)S(1)}, u32[]{:S(2)}, u32[]{:S(2)}) collective-permute-start(f32[16,512]{1,0:T(8,128)S(1)} %add.58), channel_id=1, source_target_pairs={{0,8},{4,12},{8,0},{12,4},{1,9},{5,13},{9,1},{13,5},{2,10},{6,14},... | collective-permute-start | bytes 98312 | tf_op jit(solution)/shard_map/ppermute | solution.py:42
  200.1 2.4 %collective-permute-done.3 = f32[16,512]{1,0:T(8,128)S(1)} collective-permute-done((f32[16,512]{1,0:T(8,128)S(1)}, f32[16,512]{1,0:T(8,128)S(1)}, u32[]{:S(2)}, u32[]{:S(2)}) %collective-permute-start.3) | collective-permute-done | bytes 32800 | tf_op jit(solution)/shard_map/ppermute | solution.py:42
  202.5 0.6 fusion.14
  (12 shorter events, 0.1 us)
Async XLA Ops:
  6.5 16.1 %copy-start = (bf16[512,2560]{1,0:T(8,128)(2,1)S(1)}, bf16[512,2560]{1,0:T(8,128)(2,1)}, u32[]{:S(2)}) copy-start(bf16[512,2560]{1,0:T(8,128)(2,1)} %param.13) | copy-start | bytes 7864324
  6.5 69.9 %all-reduce.5.cloned.1.call-start = ((), (), s32[]{:S(2)}) async-start(), calls=%async_computation | async-start | bytes 327680
  24.6 155.3 %all-reduce.7.cloned.1.call-start = ((), (), s32[]{:S(2)}) async-start(), calls=%async_computation.1 | async-start | bytes 1835008
  77.3 5.2 %copy-start.1 = (bf16[2,2,4096,128]{3,2,1,0:T(8,128)(2,1)S(1)}, bf16[2,2,4096,128]{3,2,1,0:T(8,128)(2,1)}, u32[]{:S(2)}) copy-start(bf16[2,2,4096,128]{3,2,1,0:T(8,128)(2,1)} %param.16) | copy-start | bytes 12582916
  82.2 21.8 %copy-start.2 = (bf16[16,512]{1,0:T(8,128)(2,1)S(1)}, bf16[16,512]{1,0:T(8,128)(2,1)}, u32[]{:S(2)}) copy-start(bf16[16,512]{1,0:T(8,128)(2,1)} %param.11) | copy-start | bytes 49156
  82.2 33.7 %copy-start.3 = (f32[512]{0:T(512)S(1)}, f32[512]{0:T(512)}, u32[]{:S(2)}) copy-start(f32[512]{0:T(512)} %param.19) | copy-start | bytes 6148
  95.3 3.9 %collective-permute-start = (f32[16,512]{1,0:T(8,128)S(1)}, f32[16,512]{1,0:T(8,128)S(1)}, u32[]{:S(2)}, u32[]{:S(2)}) collective-permute-start(f32[16,512]{1,0:T(8,128)S(1)} %fusion.37), channel_id=1, source_target_pairs={{0,4},{4,0},{8,12},{12,8},{1,5},{5,1},{9,13},{13,9},{2,6},{6,2},{1... | collective-permute-start | bytes 98312 | tf_op jit(solution)/shard_map/ppermute | solution.py:42
  99.2 4.8 %collective-permute-start.1 = (f32[16,512]{1,0:T(8,128)S(1)}, f32[16,512]{1,0:T(8,128)S(1)}, u32[]{:S(2)}, u32[]{:S(2)}) collective-permute-start(f32[16,512]{1,0:T(8,128)S(1)} %add.53), channel_id=1, source_target_pairs={{0,8},{4,12},{8,0},{12,4},{1,9},{5,13},{9,1},{13,5},{2,10},{6,14},... | collective-permute-start | bytes 98312 | tf_op jit(solution)/shard_map/ppermute | solution.py:42
  193.8 3.9 %collective-permute-start.2 = (f32[16,512]{1,0:T(8,128)S(1)}, f32[16,512]{1,0:T(8,128)S(1)}, u32[]{:S(2)}, u32[]{:S(2)}) collective-permute-start(f32[16,512]{1,0:T(8,128)S(1)} %fusion.38), channel_id=1, source_target_pairs={{0,4},{4,0},{8,12},{12,8},{1,5},{5,1},{9,13},{13,9},{2,6},{6,2},{1... | collective-permute-start | bytes 98312 | tf_op jit(solution)/shard_map/ppermute | solution.py:42
  197.7 4.8 %collective-permute-start.3 = (f32[16,512]{1,0:T(8,128)S(1)}, f32[16,512]{1,0:T(8,128)S(1)}, u32[]{:S(2)}, u32[]{:S(2)}) collective-permute-start(f32[16,512]{1,0:T(8,128)S(1)} %add.58), channel_id=1, source_target_pairs={{0,8},{4,12},{8,0},{12,4},{1,9},{5,13},{9,1},{13,5},{2,10},{6,14},... | collective-permute-start | bytes 98312 | tf_op jit(solution)/shard_map/ppermute | solution.py:42
Sparse Core Ops, SparseCore 0:
  24.7 51.6 all-reduce.4
  124.3 55.5 all-reduce.6
